TPU v7x, 128 devices: a whole 4x4x4 slice. The times are simulated.
128 devices in a mesh: row: 8 (over y, z_lo), col: 16 (over x, z_hi, core).
Axes of the slice: x: 4, y: 4, z: 4 (z_hi: 2, z_lo: 2; z = z_hi * 2 + z_lo), core: 2. Of those that a mesh axis runs over, the one named last changes fastest.
Arguments:
- view_one: bfloat16 [4096, 8192], P('row', 'col'), may hold values from -6 to 6
- view_two: bfloat16 [4096, 8192], P('row', 'col'), may hold values from -6 to 6
- pair_weights: bfloat16 [8192, 8192], P('row', 'col'), may hold values from 0.25 to 2.5
Outputs:
- first_grad: bfloat16 [4096, 8192], P('row', 'col')
- second_grad: bfloat16 [4096, 8192], P('row', 'col')
All inputs are finite; a program needn't handle non-finite values.
Results may differ from a plain program's by a relative error of at most 0.004.
Values may be sent and summed in bfloat16 or wider, within the bound.
A program may use at most 128 MiB of HBM per device.

v0:
```python
import jax
import jax.numpy as jnp
from jax import lax
from jax.sharding import Mesh
from jax.sharding import PartitionSpec as P

ROW = ("row_0", "row_1")


def whole_of(array, axes, dim):
    filled = array
    for number in range(len(axes) - 1, -1, -1):
        filled = lax.all_gather(filled, axes[number], axis=dim, tiled=True)
    return filled


def per_device(view_one, view_two, pair_weights):
    wide_two = lax.all_gather(view_two, "col", axis=1, tiled=True)
    samples = view_one.shape[0] * lax.axis_size(ROW)
    local_rows = pair_weights.shape[0]
    local_cols = pair_weights.shape[1]
    regrouped = lax.all_to_all(wide_two, ROW, split_axis=1, concat_axis=0, tiled=True)
    summed = lax.dot_general(
        regrouped,
        lax.all_gather(view_one, ROW, axis=0, tiled=True),
        (((0,), (0,)), ((), ())),
        preferred_element_type=jnp.float32,
    )
    correlation = summed / samples
    row_ids = lax.axis_index(ROW) * local_rows + lax.broadcasted_iota(
        jnp.int32, (local_rows, local_cols), 0
    )
    col_ids = lax.axis_index("col") * local_cols + lax.broadcasted_iota(
        jnp.int32, (local_rows, local_cols), 1
    )
    identity = jnp.where(row_ids == col_ids, 1.0, 0.0).astype(jnp.float32)
    weighted = (pair_weights.astype(jnp.float32) * (correlation - identity)).astype(jnp.bfloat16)
    grad_cols = whole_of(weighted, ROW, 0)
    first_grad = jnp.dot(wide_two, grad_cols, preferred_element_type=jnp.float32).astype(
        jnp.bfloat16
    )
    second_flipped = lax.psum_scatter(
        lax.dot_general(
            grad_cols, view_one, (((1,), (1,)), ((), ())), preferred_element_type=jnp.float32
        ),
        "col",
        scatter_dimension=0,
        tiled=True,
    )
    return (first_grad, second_flipped.T.astype(jnp.bfloat16))


def solution(mesh):
    torus = Mesh(mesh.devices.reshape(4, 2, mesh.shape["col"]), ("row_0", "row_1", "col"))
    placed = (P(ROW, "col"), P(ROW, "col"), P(ROW, "col"))
    return jax.shard_map(
        per_device,
        mesh=torus,
        in_specs=placed,
        out_specs=(P(ROW, "col"), P(ROW, "col")),
        check_vma=False,
    )
```

profile of v0, /device:TPU:0, one launch (start us, length us, event | category | flops | bytes accessed | tf_op | source)
XLA Modules:
  0.0 564.2 jit_solution(15220778001072842064)
XLA Ops:
  8.0 0.0 all-gather.5.cloned.1.call-start
  8.0 2.0 copy.9
  10.1 0.0 all-gather.5.cloned.1.call-update
  10.1 77.0 %all-gather.5.cloned.1.call-done = bf16[512,8192]{0,1:T(8,128)(2,1)} async-done(((bf16[512,512]{0,1:T(8,128)(2,1)}), bf16[512,8192]{0,1:T(8,128)(2,1)}) %all-gather.5.cloned.1.call-update) | async-done | bytes 8388624 | tf_op jit(solution)/shard_map/all_gather | solution.py:18
  87.1 5.0 all-to-all-start
  92.1 0.0 all-gather.7.cloned.1.call-start
  92.2 0.5 all-gather.7.cloned.1.call-update
  92.7 0.0 all-gather.9.cloned.1.call-start
  92.8 125.2 %all-to-all-done = bf16[512,8,1024]{0,2,1:T(8,128)(2,1)} async-done(((bf16[512,8,1024]{0,2,1:T(8,128)(2,1)}), bf16[512,8,1024]{0,2,1:T(8,128)(2,1)}, u32[]{:S(2)}, u32[]{:S(2)}) %all-to-all-start) | async-done | bytes 8388640 | tf_op jit(solution)/shard_map/all_to_all | solution.py:22
  218.0 0.0 copy-start.1
  218.0 11.6 %copy.10 = bf16[8,512,1024]{2,1,0:T(8,128)(2,1)} copy(bf16[8,512,1024]{1,2,0:T(8,128)(2,1)} %bitcast.1) | data formatting | bytes 16777216 | tf_op jit(solution)/shard_map/all_to_all | solution.py:22
  229.6 34.8 %all-gather.7.cloned.1.call-done = bf16[4096,512]{1,0:T(8,128)(2,1)} async-done(((bf16[512,512]{1,0:T(8,128)(2,1)}), bf16[4096,512]{1,0:T(8,128)(2,1)}) %all-gather.7.cloned.1.call-update) | async-done | bytes 4194320 | tf_op jit(solution)/shard_map/all_gather | solution.py:25
  264.4 0.0 copy-done.1
  264.4 0.0 copy-start
  264.4 10.4 %multiply_convert_fusion = bf16[1024,512]{1,0:T(8,128)(2,1)} fusion(bf16[1024,512]{1,0:T(8,128)(2,1)S(1)} %copy-done.1, bf16[4096,1024]{1,0:T(8,128)(2,1)} %bitcast.14, bf16[4096,512]{1,0:T(8,128)(2,1)} %all-gather.7.cloned.1.call-done, s32[512]{0:T(512)S(1)} %iota_add_fusion.1, s32[1024]{0:T(1024)S(1)} %iota_add_fusion), kind=kOutput, calls=%fused_computation | convolution fusion | flops 4298637312 | bytes 14686208 | tf_op jit(solution)/shard_map/dot_general | solution.py:23
  274.8 0.0 all-gather.9.cloned.1.call-update
  274.8 0.0 all-gather.11.cloned.1.call-start
  274.8 34.0 %all-gather.9.cloned.1.call-done = bf16[2048,512]{1,0:T(8,128)(2,1)} async-done(((bf16[1024,512]{1,0:T(8,128)(2,1)}), bf16[2048,512]{1,0:T(8,128)(2,1)}) %all-gather.9.cloned.1.call-update) | async-done | bytes 2097168 | tf_op jit(solution)/shard_map/all_gather | solution.py:13
  308.8 0.0 all-gather.11.cloned.1.call-update
  308.8 0.0 reduce-scatter.2.cloned.1.call-start
  308.9 85.4 %all-gather.11.cloned.1.call-done = bf16[8192,512]{1,0:T(8,128)(2,1)} async-done(((bf16[2048,512]{1,0:T(8,128)(2,1)}), bf16[8192,512]{1,0:T(8,128)(2,1)}) %all-gather.11.cloned.1.call-update) | async-done | bytes 8388624 | tf_op jit(solution)/shard_map/all_gather | solution.py:13
  394.3 0.0 copy-done
  394.3 11.7 %fusion.1 = f32[8192,512]{1,0:T(8,128)} fusion(bf16[8192,512]{1,0:T(8,128)(2,1)} %all-gather.11.cloned.1.call-done, bf16[512,512]{1,0:T(8,128)(2,1)S(1)} %copy-done), kind=kOutput, calls=%fused_computation.6 | convolution fusion | flops 4294967296 | bytes 25690112 | tf_op jit(solution)/shard_map/dot_general | solution.py:43
  405.9 0.0 reduce-scatter.2.cloned.1.call-update
  406.0 10.3 %fusion = bf16[512,512]{0,1:T(8,128)(2,1)S(1)} fusion(bf16[8192,512]{1,0:T(8,128)(2,1)} %all-gather.11.cloned.1.call-done, bf16[512,8192]{0,1:T(8,128)(2,1)} %all-gather.5.cloned.1.call-done), kind=kOutput, calls=%fused_computation.2 | convolution fusion | flops 4295229440 | bytes 17301504 | tf_op jit(solution)/shard_map/dot_general | solution.py:39
  416.2 1.0 copy.11
  417.2 137.1 %reduce-scatter.2.cloned.1.call-done = f32[512,512]{1,0:T(8,128)} async-done(((f32[8192,512]{1,0:T(8,128)}), f32[512,512]{1,0:T(8,128)}) %reduce-scatter.2.cloned.1.call-update) | async-done | bytes 1048592 | tf_op jit(solution)/shard_map/reduce_scatter | solution.py:42
  554.3 1.3 convert_bitcast_fusion
  555.6 1.0 copy.12
  (2 shorter events, 0.0 us)
Async XLA Ops:
  8.0 79.1 %all-gather.5.cloned.1.call-start = ((), (), s32[]{:S(2)}) async-start(), calls=%async_computation.2 | async-start | bytes 8912896 | tf_op jit(solution)/shard_map/all_gather | solution.py:18
  87.1 130.9 %all-to-all-start = ((bf16[512,8,1024]{0,2,1:T(8,128)(2,1)}), bf16[512,8,1024]{0,2,1:T(8,128)(2,1)}, u32[]{:S(2)}, u32[]{:S(2)}) async-start(bf16[512,8,1024]{0,2,1:T(8,128)(2,1)} %bitcast.13), calls=%async_computation | async-start | bytes 16777216 | tf_op jit(solution)/shard_map/all_to_all | solution.py:22
  92.1 172.3 %all-gather.7.cloned.1.call-start = ((), (), s32[]{:S(2)}) async-start(), calls=%async_computation.3 | async-start | bytes 4718592 | tf_op jit(solution)/shard_map/all_gather | solution.py:25
  92.7 216.1 %all-gather.9.cloned.1.call-start = ((), (), s32[]{:S(2)}) async-start(), calls=%async_computation.4 | async-start | bytes 3145728 | tf_op jit(solution)/shard_map/all_gather | solution.py:13
  218.0 46.4 %copy-start.1 = (bf16[1024,512]{1,0:T(8,128)(2,1)S(1)}, bf16[1024,512]{1,0:T(8,128)(2,1)}, u32[]{:S(2)}) copy-start(bf16[1024,512]{1,0:T(8,128)(2,1)} %param.5) | copy-start | bytes 3145732
  264.4 129.9 %copy-start = (bf16[512,512]{1,0:T(8,128)(2,1)S(1)}, bf16[512,512]{1,0:T(8,128)(2,1)}, u32[]{:S(2)}) copy-start(bf16[512,512]{1,0:T(8,128)(2,1)} %param.3) | copy-start | bytes 1572868
  274.8 119.5 %all-gather.11.cloned.1.call-start = ((), (), s32[]{:S(2)}) async-start(), calls=%async_computation.5 | async-start | bytes 10485760 | tf_op jit(solution)/shard_map/all_gather | solution.py:13
  308.8 245.5 %reduce-scatter.2.cloned.1.call-start = ((), (), s32[]{:S(2)}) async-start(), calls=%async_computation.6 | async-start | bytes 17825792 | tf_op jit(solution)/shard_map/reduce_scatter | solution.py:42
Sparse Core Ops, SparseCore 0:
  11.8 75.2 all-gather.4
  406.1 148.1 reduce-scatter.1
Sparse Core Ops, SparseCore 1:
  94.2 170.1 all-gather.6
  274.9 33.9 all-gather.8
  310.3 83.9 all-gather.10
where the time goes:
time: 565 us; the launch traced here: 564 us
  waiting for transfers between devices  494 us (87%)
  matrix products  32.3 us (6%)
  local copies, waits for them, and re-layouts  15.7 us (3%)
  between operations  15.7 us (3%)
    reduce_scatter x1, waiting for transfers between devices, per_device(): lax.psum_scatter(lax.dot_general(grad_cols, view_one, (((1,), (1,)), ((),...  137 us
    all_to_all x1, waiting for transfers between devices, per_device(): lax.all_to_all(wide_two, ROW, split_axis=1, concat_axis=0, tiled=True)  125 us
    all_gather x2, waiting for transfers between devices, whole_of(): filled = lax.all_gather(filled, axes[number], axis=dim, tiled=True)  119 us
    all_gather x1, waiting for transfers between devices, per_device(): wide_two = lax.all_gather(view_two, 'col', axis=1, tiled=True)  77 us
    all_gather x1, waiting for transfers between devices, per_device(): lax.all_gather(view_one, ROW, axis=0, tiled=True)  34.8 us
    dot_general x1, matrix products, per_device(): lax.dot_general(grad_cols, view_one, (((1,), (1,)), ((), ())), preferred_...  11.7 us
    all_to_all x1, local copies, waits for them, and re-layouts, per_device(): lax.all_to_all(wide_two, ROW, split_axis=1, concat_axis=0, tiled=True)  11.6 us
  transfers between devices with their start and end apart: 6, of which 6 were waited for; matrix products, arithmetic and copies ran while one was open for 4% of the time, Pallas kernels for 0%

commit v1 on v0

--- a/solution.py
+++ b/solution.py
@@ -19,7 +19,9 @@
     samples = view_one.shape[0] * lax.axis_size(ROW)
     local_rows = pair_weights.shape[0]
     local_cols = pair_weights.shape[1]
-    regrouped = lax.all_to_all(wide_two, ROW, split_axis=1, concat_axis=0, tiled=True)
+    shards = jnp.split(wide_two, lax.axis_size(ROW), axis=1)
+    incoming = lax.all_to_all(jnp.stack(shards), ROW, 0, 0)
+    regrouped = jnp.concatenate(incoming, axis=0)
     summed = lax.dot_general(
         regrouped,
         lax.all_gather(view_one, ROW, axis=0, tiled=True),

time: 565 us -> 574 us (1.016)
  waiting for transfers between devices: 494 us -> 500 us
    all_to_all x1, waiting for transfers between devices: 125 us -> 0.01 us  [per_device(): incoming = lax.all_to_all(jnp.stack(shards), ROW, 0, 0)]
    all_gather x1, waiting for transfers between devices: 34.8 us -> 156 us  [per_device(): lax.all_gather(view_one, ROW, axis=0, tiled=True)]
    unnamed x7 -> x13, local copies, waits for them, and re-layouts: 4.06 us -> 18.1 us
    all_to_all x1 -> x0, local copies, waits for them, and re-layouts: 11.6 us -> none  [per_device(): lax.all_to_all(wide_two, ROW, split_axis=1, concat_axis=0, tiled=True)]
    all_gather x1, waiting for transfers between devices: 77 us -> 83.3 us  [per_device(): wide_two = lax.all_gather(view_two, 'col', axis=1, tiled=True)]
  transfers between devices with their start and end apart: 6 -> 6, of which waited for: 6 -> 5; matrix products, arithmetic and copies ran while one was open for 4% -> 5% of each run, Pallas kernels for 0% -> 0%
where the time goes in v1:
time: 574 us; the launch traced here: 573 us
  waiting for transfers between devices  500 us (87%)
  matrix products  32.3 us (6%)
  local copies, waits for them, and re-layouts  20.4 us (4%)
  between operations  13.8 us (2%)
    all_gather x1, waiting for transfers between devices, per_device(): lax.all_gather(view_one, ROW, axis=0, tiled=True)  156 us
    reduce_scatter x1, waiting for transfers between devices, per_device(): lax.psum_scatter(lax.dot_general(grad_cols, view_one, (((1,), (1,)), ((),...  137 us
    all_gather x2, waiting for transfers between devices, whole_of(): filled = lax.all_gather(filled, axes[number], axis=dim, tiled=True)  122 us
    all_gather x1, waiting for transfers between devices, per_device(): wide_two = lax.all_gather(view_two, 'col', axis=1, tiled=True)  83.3 us
    unnamed x13, local copies, waits for them, and re-layouts  18.1 us
    dot_general x1, matrix products, per_device(): lax.dot_general(grad_cols, view_one, (((1,), (1,)), ((), ())), preferred_...  11.7 us
  transfers between devices with their start and end apart: 6, of which 5 were waited for; matrix products, arithmetic and copies ran while one was open for 5% of the time, Pallas kernels for 0%

profile of v1, /device:TPU:0, one launch (start us, length us, event | category | flops | bytes accessed | tf_op | source)
XLA Modules:
  0.0 573.1 jit_solution(801182867494010707)
XLA Ops:
  7.2 0.0 all-gather.5.cloned.1.call-start
  7.2 0.7 all-gather.5.cloned.1.call-update
  7.9 0.0 all-gather.7.cloned.1.call-start
  7.9 0.7 all-gather.7.cloned.1.call-update
  8.6 83.3 %all-gather.5.cloned.1.call-done = bf16[512,8192]{1,0:T(8,128)(2,1)} async-done(((bf16[512,512]{1,0:T(8,128)(2,1)}), bf16[512,8192]{1,0:T(8,128)(2,1)}) %all-gather.5.cloned.1.call-update) | async-done | bytes 8388624 | tf_op jit(solution)/shard_map/all_gather | solution.py:18
  91.9 2.4 fusion.8
  94.3 2.3 fusion.7
  96.6 2.3 fusion.6
  98.8 2.3 fusion.5
  101.1 2.3 fusion.4
  103.5 2.3 fusion.3
  105.7 2.3 fusion.2
  108.0 2.3 fusion.1
  110.3 5.1 all-to-all-start
  115.4 0.0 all-gather.9.cloned.1.call-start
  115.4 156.0 %all-gather.7.cloned.1.call-done = bf16[4096,512]{1,0:T(8,128)(2,1)} async-done(((bf16[512,512]{1,0:T(8,128)(2,1)}), bf16[4096,512]{1,0:T(8,128)(2,1)}) %all-gather.7.cloned.1.call-update) | async-done | bytes 4194320 | tf_op jit(solution)/shard_map/all_gather | solution.py:27
  271.5 0.0 all-to-all-done
  271.5 0.0 copy-done.1
  271.5 10.4 %multiply_convert_fusion = bf16[1024,512]{1,0:T(8,128)(2,1)} fusion(bf16[1024,512]{1,0:T(8,128)(2,1)S(1)} %copy-done.1, bf16[4096,1024]{1,0:T(8,128)(2,1)} %bitcast.8, bf16[4096,512]{1,0:T(8,128)(2,1)} %all-gather.7.cloned.1.call-done, s32[512]{0:T(512)S(1)} %iota_add_fusion.1, s32[1024]{0:T(1024)S(1)} %iota_add_fusion), kind=kOutput, calls=%fused_computation | convolution fusion | flops 4298637312 | bytes 14686208 | tf_op jit(solution)/shard_map/dot_general | solution.py:25
  281.8 0.0 all-gather.9.cloned.1.call-update
  281.9 0.0 all-gather.11.cloned.1.call-start
  281.9 36.7 %all-gather.9.cloned.1.call-done = bf16[2048,512]{1,0:T(8,128)(2,1)} async-done(((bf16[1024,512]{1,0:T(8,128)(2,1)}), bf16[2048,512]{1,0:T(8,128)(2,1)}) %all-gather.9.cloned.1.call-update) | async-done | bytes 2097168 | tf_op jit(solution)/shard_map/all_gather | solution.py:13
  318.6 0.0 all-gather.11.cloned.1.call-update
  318.7 0.2 reduce-scatter.2.cloned.1.call-start
  318.9 85.4 %all-gather.11.cloned.1.call-done = bf16[8192,512]{1,0:T(8,128)(2,1)} async-done(((bf16[2048,512]{1,0:T(8,128)(2,1)}), bf16[8192,512]{1,0:T(8,128)(2,1)}) %all-gather.11.cloned.1.call-update) | async-done | bytes 8388624 | tf_op jit(solution)/shard_map/all_gather | solution.py:13
  404.2 11.7 %fusion.9 = f32[8192,512]{1,0:T(8,128)} fusion(bf16[8192,512]{1,0:T(8,128)(2,1)} %all-gather.11.cloned.1.call-done, bf16[512,512]{1,0:T(8,128)(2,1)S(1)} %copy-done), kind=kOutput, calls=%fused_computation.22 | convolution fusion | flops 4294967296 | bytes 25690112 | tf_op jit(solution)/shard_map/dot_general | solution.py:45
  415.9 0.0 reduce-scatter.2.cloned.1.call-update
  415.9 10.3 %fusion = bf16[512,512]{0,1:T(8,128)(2,1)S(1)} fusion(bf16[8192,512]{1,0:T(8,128)(2,1)} %all-gather.11.cloned.1.call-done, bf16[512,8192]{1,0:T(8,128)(2,1)} %all-gather.5.cloned.1.call-done), kind=kOutput, calls=%fused_computation.2 | convolution fusion | flops 4295229440 | bytes 17301504 | tf_op jit(solution)/shard_map/dot_general | solution.py:41
  426.2 1.0 copy.5
  427.2 137.1 %reduce-scatter.2.cloned.1.call-done = f32[512,512]{1,0:T(8,128)} async-done(((f32[8192,512]{1,0:T(8,128)}), f32[512,512]{1,0:T(8,128)}) %reduce-scatter.2.cloned.1.call-update) | async-done | bytes 1048592 | tf_op jit(solution)/shard_map/reduce_scatter | solution.py:44
  564.3 1.3 convert_bitcast_fusion
  565.6 1.0 copy.6
  (5 shorter events, 0.0 us)
Async XLA Ops:
  7.2 84.8 %all-gather.5.cloned.1.call-start = ((), (), s32[]{:S(2)}) async-start(), calls=%async_computation.2 | async-start | bytes 8912896 | tf_op jit(solution)/shard_map/all_gather | solution.py:18
  7.9 263.6 %all-gather.7.cloned.1.call-start = ((), (), s32[]{:S(2)}) async-start(), calls=%async_computation.3 | async-start | bytes 4718592 | tf_op jit(solution)/shard_map/all_gather | solution.py:27
  110.3 161.2 %copy-start.1 = (bf16[1024,512]{1,0:T(8,128)(2,1)S(1)}, bf16[1024,512]{1,0:T(8,128)(2,1)}, u32[]{:S(2)}) copy-start(bf16[1024,512]{1,0:T(8,128)(2,1)} %param.5) | copy-start | bytes 3145732
  110.3 161.2 %all-to-all-start = ((bf16[8,512,1024]{2,1,0:T(8,128)(2,1)}), bf16[8,512,1024]{2,1,0:T(8,128)(2,1)}, u32[]{:S(2)}, u32[]{:S(2)}) async-start(bf16[8,512,1024]{2,1,0:T(8,128)(2,1)} %fusion.1), calls=%async_computation | async-start | bytes 16777216 | tf_op jit(solution)/shard_map/all_to_all | solution.py:23
  115.4 203.3 %all-gather.9.cloned.1.call-start = ((), (), s32[]{:S(2)}) async-start(), calls=%async_computation.4 | async-start | bytes 3145728 | tf_op jit(solution)/shard_map/all_gather | solution.py:13
  271.5 132.8 %copy-start = (bf16[512,512]{1,0:T(8,128)(2,1)S(1)}, bf16[512,512]{1,0:T(8,128)(2,1)}, u32[]{:S(2)}) copy-start(bf16[512,512]{1,0:T(8,128)(2,1)} %param.3) | copy-start | bytes 1572868
  281.9 122.4 %all-gather.11.cloned.1.call-start = ((), (), s32[]{:S(2)}) async-start(), calls=%async_computation.5 | async-start | bytes 10485760 | tf_op jit(solution)/shard_map/all_gather | solution.py:13
  318.7 245.6 %reduce-scatter.2.cloned.1.call-start = ((), (), s32[]{:S(2)}) async-start(), calls=%async_computation.6 | async-start | bytes 17825792 | tf_op jit(solution)/shard_map/reduce_scatter | solution.py:44
Sparse Core Ops, SparseCore 0:
  10.2 81.6 all-gather.4
  93.6 177.8 all-gather.6
  282.0 36.6 all-gather.8
  320.2 84.0 all-gather.10
  416.0 148.2 reduce-scatter.1
